TPU v7x, 32 devices: a whole 2x2x4 slice. The times are simulated.
32 devices in a mesh: seq: 2 (over core), width: 4 (over y, x), dp: 4 (over z).
Axes of the slice: x: 2, y: 2, z: 4, core: 2. Of those that a mesh axis runs over, the one named last changes fastest.
Arguments:
- inputs: bfloat16 [4, 512, 5376], P('dp', 'seq', 'width'), may hold values from -6 to 6
- out_grad: bfloat16 [4, 512, 5376], P('dp', 'seq', 'width'), may hold values from -6 to 6
- gate_a: bfloat16 [16, 336, 336], P('width'), may hold values from -0.3125 to 0.3125
- gate_x: bfloat16 [16, 336, 336], P('width'), may hold values from -0.3125 to 0.3125
- bias_a: float32 [5376], P('width'), may hold values from -1.5 to 1.5
- bias_x: float32 [5376], P('width'), may hold values from -1.5 to 1.5
- decay_param: float32 [5376], P('width'), may hold values from -12 to -4.5
- segment_ids: int32 [4, 512], P('dp', 'seq'), may hold values from 0 to 3, never falling along the last dimension, each value on 1 to 256 neighbouring positions
Outputs:
- input_grad: bfloat16 [4, 512, 5376], P('dp', 'seq', 'width')
- gate_a_grad: float32 [16, 336, 336], P('width')
- gate_x_grad: float32 [16, 336, 336], P('width')
- bias_a_grad: float32 [5376], P('width')
- bias_x_grad: float32 [5376], P('width')
- decay_grad: float32 [5376], P('width')
All inputs are finite; a program needn't handle non-finite values.
Results may differ from a plain program's by a relative error of at most 0.0029.
Values sent between devices are 32-bit elements; how exact they have to be, the bound alone decides.
No kernel may reach another device: no remote copies, remote signals or barrier semaphores. Data moves between devices by JAX's collectives and lax.ppermute only.
A program may use at most 128 MiB of HBM per device.

v0:
```python
import jax
import jax.numpy as jnp
from jax import lax
from jax.sharding import PartitionSpec as P


def shifted(value, axis, steps):
    count = lax.axis_size(axis)
    initial, last = (max(0, -steps), min(count, count - steps))
    return lax.ppermute(value, axis, [(source, source + steps) for source in range(initial, last)])


def carried_in(value, axis, join, neutral, backward):
    count, mine = (lax.axis_size(axis), lax.axis_index(axis))
    pieces = jax.tree.map(lambda part: lax.all_gather(part, axis), value)
    if backward:
        pieces = jax.tree.map(lambda part: part[::-1], pieces)
        mine = count - 1 - mine
    running = jax.tree.map(
        lambda part, zero: jnp.full_like(part, 0) + jnp.asarray(zero, part.dtype), value, neutral
    )

    def hop(position, running):
        longer = join(running, jax.tree.map(lambda part: part[position], pieces))
        return jax.tree.map(lambda new, old: jnp.where(position < mine, new, old), longer, running)

    return lax.fori_loop(0, count - 1, hop, running)


def combine(earlier, later):
    return (earlier[0] * later[0], earlier[1] * later[0] + later[1])


def shards(inputs, out_grad, gate_a, gate_x, bias_a, bias_x, decay_param, segment_ids):
    batch, count, chans = inputs.shape
    blocks, width_k = (gate_a.shape[0], gate_a.shape[1])
    span_len = 8
    groups = count // span_len
    blocked = inputs.reshape(batch, count, blocks, width_k)
    pre_a = (
        jnp.einsum("stbk,bkj->stbj", blocked, gate_a, preferred_element_type=jnp.float32).reshape(
            batch, count, chans
        )
        + bias_a
    )
    pre_x = (
        jnp.einsum("stbk,bkj->stbj", blocked, gate_x, preferred_element_type=jnp.float32).reshape(
            batch, count, chans
        )
        + bias_x
    )
    rate = jax.nn.sigmoid(pre_a)
    ingate = jax.nn.sigmoid(pre_x)
    soft = jax.nn.softplus(decay_param)
    log_a = -8.0 * rate * soft
    decay = jnp.exp(log_a)
    shifted_ids = segment_ids + 1
    before = shifted(shifted_ids[:, -1:], "seq", 1)
    previous = jnp.concatenate([before, shifted_ids[:, :-1]], 1)
    position = lax.axis_index("seq") * count + jnp.arange(count, dtype=jnp.int32)
    reset = (shifted_ids != previous) | (position[None, :] == 0)
    keep = jnp.where(reset, 0.0, 1.0).astype(jnp.float32)[:, :, None]
    abar = keep * decay
    mult = jnp.where(keep > 0.5, jnp.sqrt(-jnp.expm1(2.0 * log_a)), 1.0)
    xf = inputs.astype(jnp.float32)
    dyf = out_grad.astype(jnp.float32)
    drive = mult * ingate * xf
    cum_log = jnp.cumsum(log_a.reshape(batch, groups, span_len, chans), 2)
    cum_reset = jnp.cumsum(
        jnp.where(reset, 1.0, 0.0).astype(jnp.float32).reshape(batch, groups, span_len), 2
    )
    order = jnp.arange(span_len, dtype=jnp.int32)
    lower = order[:, None] >= order[None, :]
    linked = (cum_reset[:, :, :, None] == cum_reset[:, :, None, :]) & lower
    spread = cum_log[:, :, :, None, :] - cum_log[:, :, None, :, :]
    factor = jnp.where(linked[..., None], jnp.exp(jnp.minimum(spread, 0.0)), 0.0)
    state_loc = jnp.einsum(
        "bntsc,bnsc->bntc",
        factor,
        drive.reshape(batch, groups, span_len, chans),
        precision=lax.Precision.HIGHEST,
    )
    grad_loc = jnp.einsum(
        "bntsc,bntc->bnsc",
        factor,
        dyf.reshape(batch, groups, span_len, chans),
        precision=lax.Precision.HIGHEST,
    )
    from_start = jnp.exp(cum_log) * jnp.where(cum_reset == 0.0, 1.0, 0.0)[..., None]
    to_end = (
        jnp.exp(cum_log[:, :, -1:, :] - cum_log)
        * jnp.where(cum_reset == cum_reset[:, :, -1:], 1.0, 0.0)[..., None]
    )
    group_prod = from_start[:, :, -1]
    group_state = state_loc[:, :, -1]
    group_grad = abar.reshape(batch, groups, span_len, chans)[:, :, 0] * grad_loc[:, :, 0]
    fwd_p, fwd_s = lax.associative_scan(combine, (group_prod, group_state), axis=1)
    bwd_p, bwd_s = lax.associative_scan(combine, (group_prod, group_grad), reverse=True, axis=1)
    forward_sum = (fwd_p[:, -1], fwd_s[:, -1])
    backward_sum = (bwd_p[:, 0], bwd_s[:, 0])
    unit = jnp.ones((batch, chans), jnp.float32)
    naught = jnp.zeros((batch, chans), jnp.float32)
    state_in = carried_in(forward_sum, "seq", combine, (unit, naught), False)[1]
    grad_in = carried_in(backward_sum, "seq", combine, (unit, naught), True)[1]
    excl_p = jnp.concatenate([unit[:, None], fwd_p[:, :-1]], 1)
    excl_s = jnp.concatenate([naught[:, None], fwd_s[:, :-1]], 1)
    entering = excl_s + excl_p * state_in[:, None, :]
    later_p = jnp.concatenate([bwd_p[:, 1:], unit[:, None]], 1)
    later_s = jnp.concatenate([bwd_s[:, 1:], naught[:, None]], 1)
    leaving = later_s + later_p * grad_in[:, None, :]
    state = (state_loc + from_start * entering[:, :, None, :]).reshape(batch, count, chans)
    grad = (grad_loc + to_end * leaving[:, :, None, :]).reshape(batch, count, chans)
    wsum = grad * (state - drive) - keep * (grad * ingate * xf * decay * decay / mult)
    dpre_a = -8.0 * soft * rate * (1.0 - rate) * wsum
    dpre_x = grad * mult * xf * ingate * (1.0 - ingate)
    da_b = dpre_a.astype(jnp.bfloat16).reshape(batch, count, blocks, width_k)
    dx_b = dpre_x.astype(jnp.bfloat16).reshape(batch, count, blocks, width_k)
    back = jnp.einsum(
        "stbj,bkj->stbk", da_b, gate_a, preferred_element_type=jnp.float32
    ) + jnp.einsum("stbj,bkj->stbk", dx_b, gate_x, preferred_element_type=jnp.float32)
    input_grad = (grad * mult * ingate + back.reshape(batch, count, chans)).astype(jnp.bfloat16)
    local_a = jnp.einsum("stbk,stbj->bkj", blocked, da_b, preferred_element_type=jnp.float32)
    local_x = jnp.einsum("stbk,stbj->bkj", blocked, dx_b, preferred_element_type=jnp.float32)
    bias_ga = jnp.sum(dpre_a, (0, 1))
    bias_gx = jnp.sum(dpre_x, (0, 1))
    decay_g = jnp.sum(-8.0 * rate * wsum, (0, 1))
    grad_a, grad_x, bias_ga, bias_gx, decay_g = lax.psum(
        (local_a, local_x, bias_ga, bias_gx, decay_g), ("seq", "dp")
    )
    return (input_grad, grad_a, grad_x, bias_ga, bias_gx, jax.nn.sigmoid(decay_param) * decay_g)


def solution(mesh):
    in_specs = (
        P("dp", "seq", "width"),
        P("dp", "seq", "width"),
        P("width", None, None),
        P("width", None, None),
        P("width"),
        P("width"),
        P("width"),
        P("dp", "seq"),
    )
    out_specs = (
        P("dp", "seq", "width"),
        P("width", None, None),
        P("width", None, None),
        P("width"),
        P("width"),
        P("width"),
    )
    return jax.shard_map(shards, mesh=mesh, in_specs=in_specs, out_specs=out_specs, check_vma=False)
```

profile of v0, /device:TPU:0, one launch (start us, length us, event | category | flops | bytes accessed | tf_op | source)
XLA Modules:
  0.0 415.5 jit_solution(12818486162488649593)
XLA Ops:
  28.6 6.4 %reduce_window_sum.23 = f32[1,32,8,1344]{3,2,1,0:T(8,128)S(1)} reduce-window(f32[1,32,8,1344]{3,2,1,0:T(8,128)} %divide_multiply_fusion, f32[]{:T(128)} %constant.20.clone.1), window={size=1x1x8x1 pad=0_0x0_0x7_0x0_0}, to_apply=%region_1.2 | reduce-window | flops 2408448 | bytes 2752516 | tf_op jit(solution)/shard_map/jit(cumsum)/reduce_window_sum | solution.py:68
  37.2 4.8 %multiply_reduce_fusion.1 = f32[32,1344,8]{1,2,0:T(8,128)S(1)} fusion(f32[32,1344,8]{1,2,0:T(8,128)} %bitcast_convert_fusion, f32[32,8,1344]{2,1,0:T(8,128)S(1)} %bitcast.111, pred[32,8,8]{2,1,0:T(8,128)(4,1)S(1)} %compare_and_fusion), kind=kLoop, calls=%fused_computation.1 | loop fusion | flops 13418496 | bytes 4130816 | tf_op jit(solution)/shard_map/bntsc,bntc->bnsc/dot_general | solution.py:83
  47.9 15.7 %multiply_reduce_fusion = f32[32,1344,8]{1,2,0:T(8,128)S(1)} fusion(f32[32,1344,8]{1,2,0:T(8,128)S(1)} %fusion.6, f32[32,8,1344]{2,1,0:T(8,128)S(1)} %bitcast.112, pred[32,8,8]{2,1,0:T(8,128)(4,1)S(1)} %compare_and_fusion), kind=kLoop, calls=%fused_computation | loop fusion | flops 13418496 | bytes 4130816 | tf_op jit(solution)/shard_map/bntsc,bnsc->bntc/dot_general | solution.py:77
  87.1 3.2 pad.142
  91.6 3.2 pad.132
  94.8 3.2 pad.133
  98.0 3.2 pad.143
  127.6 3.2 pad.162
  132.2 3.2 pad.152
  135.4 3.2 pad.153
  138.6 3.2 pad.163
  147.7 4.7 %pad.164 = f32[1,16,1344]{2,0,1:T(1,128)} pad(f32[1,8,1344]{2,0,1:T(1,128)} %pad_maximum_fusion.7, f32[]{:T(128)} %constant.20.clone.1), padding=0_0_0x0_1_1x0_0_0 | pad | bytes 129028 | tf_op jit(solution)/shard_map/pad | solution.py:97
  153.8 4.7 %pad.154 = f32[1,16,1344]{2,0,1:T(1,128)} pad(f32[1,8,1344]{2,0,1:T(1,128)} %pad_maximum_fusion.6, f32[]{:T(128)} %constant.20.clone.1), padding=0_0_0x0_1_1x0_0_0 | pad | bytes 129028 | tf_op jit(solution)/shard_map/pad | solution.py:97
  158.4 4.7 %pad.155 = f32[1,16,1344]{2,0,1:T(1,128)} pad(f32[1,8,1344]{2,0,1:T(1,128)} %add.512, f32[]{:T(128)} %constant.20.clone.1), padding=0_0_0x1_0_1x0_0_0 | pad | bytes 129028 | tf_op jit(solution)/shard_map/pad | solution.py:97
  163.1 4.7 %pad.165 = f32[1,16,1344]{2,0,1:T(1,128)} pad(f32[1,8,1344]{2,0,1:T(1,128)} %add.519, f32[]{:T(128)} %constant.20.clone.1), padding=0_0_0x1_0_1x0_0_0 | pad | bytes 129028 | tf_op jit(solution)/shard_map/pad | solution.py:97
  172.4 5.6 %pad.307 = f32[1,31,1344]{2,0,1:T(1,128)} pad(f32[1,16,1344]{2,0,1:T(1,128)S(1)} %add.520, f32[]{:T(128)} %constant.20.clone.1), padding=0_0_0x0_0_1x0_0_0 | pad | bytes 252676
  178.0 5.6 %pad.167 = f32[1,32,1344]{2,0,1:T(1,128)} pad(f32[1,16,1344]{2,0,1:T(1,128)S(1)} %add.520, f32[]{:T(128)} %constant.20.clone.1), padding=0_0_0x1_0_1x0_0_0 | pad | bytes 258052 | tf_op jit(solution)/shard_map/pad | solution.py:97
  183.5 8.4 %pad.305 = f32[1,31,1344]{2,0,1:T(1,128)} pad(f32[1,16,1344]{2,0,1:T(1,128)} %add.514, f32[]{:T(128)} %constant.20.clone.1), padding=0_0_0x0_0_1x0_0_0 | pad | bytes 252676
  192.0 8.4 %pad.157 = f32[1,32,1344]{2,0,1:T(1,128)} pad(f32[1,16,1344]{2,0,1:T(1,128)} %add.514, f32[]{:T(128)} %constant.20.clone.1), padding=0_0_0x1_0_1x0_0_0 | pad | bytes 258052 | tf_op jit(solution)/shard_map/pad | solution.py:97
  201.7 5.6 %pad.309 = f32[1,31,1344]{2,0,1:T(1,128)} pad(f32[1,16,1344]{2,0,1:T(1,128)S(1)} %add.486, f32[]{:T(128)} %constant.20.clone.1), padding=0_0_0x0_0_1x0_0_0 | pad | bytes 252676
  207.2 5.5 %pad.137 = f32[1,32,1344]{2,0,1:T(1,128)} pad(f32[1,16,1344]{2,0,1:T(1,128)S(1)} %add.486, f32[]{:T(128)} %constant.20.clone.1), padding=0_0_0x1_0_1x0_0_0 | pad | bytes 258052 | tf_op jit(solution)/shard_map/pad | solution.py:98
  213.7 4.7 %pad.145 = f32[1,16,1344]{2,0,1:T(1,128)} pad(f32[1,8,1344]{2,0,1:T(1,128)} %add.491, f32[]{:T(128)} %constant.20.clone.1), padding=0_0_0x1_0_1x0_0_0 | pad | bytes 129028 | tf_op jit(solution)/shard_map/pad | solution.py:98
  219.4 5.6 %pad.311 = f32[1,31,1344]{2,0,1:T(1,128)} pad(f32[1,16,1344]{2,0,1:T(1,128)S(1)} %add.492, f32[]{:T(128)} %constant.20.clone.1), padding=0_0_0x0_0_1x0_0_0 | pad | bytes 252676
  225.0 5.6 %pad.147 = f32[1,32,1344]{2,0,1:T(1,128)} pad(f32[1,16,1344]{2,0,1:T(1,128)S(1)} %add.492, f32[]{:T(128)} %constant.20.clone.1), padding=0_0_0x1_0_1x0_0_0 | pad | bytes 258052 | tf_op jit(solution)/shard_map/pad | solution.py:98
  231.5 5.6 %pad.156 = f32[1,32,1344]{2,0,1:T(1,128)} pad(f32[1,16,1344]{2,0,1:T(1,128)S(1)} %pad_maximum_fusion.2, f32[]{:T(128)} %constant.20.clone.1), padding=0_0_0x0_1_1x0_0_0 | pad | bytes 258052 | tf_op jit(solution)/shard_map/pad | solution.py:97
  238.1 5.5 %pad.166 = f32[1,32,1344]{2,0,1:T(1,128)} pad(f32[1,16,1344]{2,0,1:T(1,128)S(1)} %pad_maximum_fusion.3, f32[]{:T(128)} %constant.20.clone.1), padding=0_0_0x0_1_1x0_0_0 | pad | bytes 258052 | tf_op jit(solution)/shard_map/pad | solution.py:97
  246.9 8.5 %pad.146 = f32[1,32,1344]{2,0,1:T(1,128)} pad(f32[1,16,1344]{2,0,1:T(1,128)} %pad_maximum_fusion.1, f32[]{:T(128)} %constant.20.clone.1), padding=0_0_0x0_1_1x0_0_0 | pad | bytes 258052 | tf_op jit(solution)/shard_map/pad | solution.py:98
  257.0 8.4 %pad.136 = f32[1,32,1344]{2,0,1:T(1,128)} pad(f32[1,16,1344]{2,0,1:T(1,128)} %pad_maximum_fusion, f32[]{:T(128)} %constant.20.clone.1), padding=0_0_0x0_1_1x0_0_0 | pad | bytes 258052 | tf_op jit(solution)/shard_map/pad | solution.py:98
  284.3 7.3 %fusion.15 = (f32[1344]{0:T(1024)}, f32[1,256,1344]{2,1,0:T(8,128)S(1)}, f32[1344]{0:T(1024)}, f32[1344]{0:T(1024)}, f32[1,256,1344]{2,1,0:T(8,128)}) fusion(bf16[1,256,1344]{2,1,0:T(8,128)(2,1)} %copy.78, f32[1,256,1344]{2,1,0:T(8,128)} %copy.77, f32[1344]{0:T(1024)} %param.13, f32[1344]{0:T(1024)S(1)} %fusion.19, f32[1,256,1344]{2,1,0:T(8,128)} %copy.75, ...), kind=kLoop, calls=%fused_computation.84 | loop fusion | flops 15134784 | bytes 10873600 | tf_op jit(solution)/shard_map/reduce_sum | solution.py:125
  310.0 3.3 add_convert_fusion
  315.6 33.0 %all-reduce.44 = (f32[1344]{0:T(1024)}, f32[1344]{0:T(1024)}, f32[1344]{0:T(1024)S(1)}) all-reduce(f32[1344]{0:T(1024)S(1)} %copy-done.35, f32[1344]{0:T(1024)S(1)} %copy-done.34, f32[1344]{0:T(1024)S(1)} %copy-done.36), channel_id=1, replica_groups=mesh['seq'=2,'width'=4,'dp'=4] {'seq','dp'}, use_global_device_ids=true, to_apply=%region_5.6 | all-reduce | flops 4032 | bytes 32256 | tf_op jit(solution)/shard_map/psum | solution.py:127
  349.2 53.6 %all-reduce.48.cloned.1.call-done = (f32[4,336,336]{1,2,0:T(8,128)}, f32[4,336,336]{1,2,0:T(8,128)}) async-done(((f32[4,336,336]{1,2,0:T(8,128)}, f32[4,336,336]{1,2,0:T(8,128)}), (f32[4,336,336]{1,2,0:T(8,128)}, f32[4,336,336]{1,2,0:T(8,128)})) %all-reduce.48.cloned.1.call-update) | async-done | bytes 3612688 | tf_op jit(solution)/shard_map/psum | solution.py:127
  (224 shorter events, 149.5 us)
Async XLA Ops:
  7.2 8.9 %copy-start = (bf16[4,336,336]{2,1,0:T(8,128)(2,1)S(1)}, bf16[4,336,336]{2,1,0:T(8,128)(2,1)}, u32[]{:S(2)}) copy-start(bf16[4,336,336]{2,1,0:T(8,128)(2,1)} %param.10) | copy-start | bytes 2709508
  7.2 7.3 %copy-start.21 = (bf16[1,256,1344]{1,2,0:T(8,128)(2,1)S(1)}, bf16[1,256,1344]{1,2,0:T(8,128)(2,1)}, u32[]{:S(2)}) copy-start(bf16[1,256,1344]{1,2,0:T(8,128)(2,1)} %param.9) | copy-start | bytes 2064388
  7.2 395.6 %all-reduce.48.cloned.1.call-start = ((), (), s32[]{:S(2)}) async-start(), calls=%async_computation | async-start | bytes 8257536 | tf_op jit(solution)/shard_map/psum | solution.py:127
  8.6 27.3 %collective-permute-start = (s32[1,1]{1,0:T(1,128)}, s32[1,1]{1,0:T(1,128)}, u32[]{:S(2)}, u32[]{:S(2)}) collective-permute-start(s32[1,1]{1,0:T(1,128)} %slice.468), channel_id=1, source_target_pairs={{0,16},{1,17},{2,18},{3,19},{4,20},{5,21},{6,22},{7,23},{8,24},{9,... | collective-permute-start | bytes 20 | tf_op jit(solution)/shard_map/ppermute | solution.py:10
  28.6 7.3 %copy-start.41 = (s32[1,256]{1,0:T(1,128)S(1)}, s32[1,256]{1,0:T(1,128)}, u32[]{:S(2)}) copy-start(s32[1,256]{1,0:T(1,128)} %param.15) | copy-start | bytes 3076
  36.5 9.0 %copy-start.40 = (f32[1,256]{1,0:T(1,128)}, f32[1,256]{1,0:T(1,128)S(1)}, u32[]{:S(2)}) copy-start(f32[1,256]{1,0:T(1,128)S(1)} %get-tuple-element.78) | copy-start | bytes 3076
  37.2 9.1 %copy-start.1 = (f32[1,256,1344]{2,1,0:T(8,128)S(1)}, f32[1,256,1344]{2,1,0:T(8,128)}, u32[]{:S(2)}) copy-start(f32[1,256,1344]{2,1,0:T(8,128)} %copy.77) | copy-start | bytes 4128772
  37.2 9.1 %copy-start.4 = (f32[1,256,1344]{2,1,0:T(8,128)S(1)}, f32[1,256,1344]{2,1,0:T(8,128)}, u32[]{:S(2)}) copy-start(f32[1,256,1344]{2,1,0:T(8,128)} %copy.75) | copy-start | bytes 4128772
  37.2 9.1 %copy-start.31 = (f32[1344]{0:T(1024)S(1)}, f32[1344]{0:T(1024)}, u32[]{:S(2)}) copy-start(f32[1344]{0:T(1024)} %param.13) | copy-start | bytes 16132
  42.0 4.3 %copy-start.8 = (bf16[1,256,1344]{2,1,0:T(8,128)(2,1)S(1)}, bf16[1,256,1344]{2,1,0:T(8,128)(2,1)}, u32[]{:S(2)}) copy-start(bf16[1,256,1344]{2,1,0:T(8,128)(2,1)} %copy.78) | copy-start | bytes 2064388
  44.8 3.1 copy-start.15
  45.6 2.3 copy-start.42
  112.5 39.9 %copy-start.39 = (f32[1,1,1344]{2,0,1:T(1,128)S(1)}, f32[1,1,1344]{2,0,1:T(1,128)}, u32[]{:S(2)}) copy-start(f32[1,1,1344]{2,0,1:T(1,128)} %slice.512) | copy-start | bytes 16132
  171.4 30.0 %copy-start.28 = (f32[1,8,1344]{2,0,1:T(1,128)S(1)}, f32[1,8,1344]{2,0,1:T(1,128)}, u32[]{:S(2)}) copy-start(f32[1,8,1344]{2,0,1:T(1,128)} %add.484) | copy-start | bytes 129028
  171.4 41.4 %copy-start.38 = (f32[1,1,1344]{2,0,1:T(1,128)S(1)}, f32[1,1,1344]{2,0,1:T(1,128)}, u32[]{:S(2)}) copy-start(f32[1,1,1344]{2,0,1:T(1,128)} %slice.496) | copy-start | bytes 16132
  218.4 36.9 %slice-start = ((f32[1,32,1344]{2,0,1:T(1,128)}), f32[1,1,1344]{2,0,1:T(1,128)S(1)}, s32[]{:S(2)}) async-start(f32[1,32,1344]{2,0,1:T(1,128)} %copy-done.15), calls=%async_computation.1 | async-start | bytes 11264 | tf_op jit(solution)/shard_map/slice | solution.py:98
  245.4 31.7 %copy-start.17 = (f32[1,32,1344]{2,0,1:T(1,128)S(1)}, f32[1,32,1344]{2,0,1:T(1,128)}, u32[]{:S(2)}) copy-start(f32[1,32,1344]{2,0,1:T(1,128)} %pad.167) | copy-start | bytes 516100
  245.4 32.8 %copy-start.18 = (f32[1,32,1344]{2,0,1:T(1,128)S(1)}, f32[1,32,1344]{2,0,1:T(1,128)}, u32[]{:S(2)}) copy-start(f32[1,32,1344]{2,0,1:T(1,128)} %pad.157) | copy-start | bytes 516100
  268.8 10.9 %copy-start.19 = (f32[1,32,1344]{2,0,1:T(1,128)S(1)}, f32[1,32,1344]{2,0,1:T(1,128)}, u32[]{:S(2)}) copy-start(f32[1,32,1344]{2,0,1:T(1,128)} %pad.147) | copy-start | bytes 516100
  268.8 10.9 %copy-start.20 = (f32[1,32,1344]{2,0,1:T(1,128)S(1)}, f32[1,32,1344]{2,0,1:T(1,128)}, u32[]{:S(2)}) copy-start(f32[1,32,1344]{2,0,1:T(1,128)} %pad.146) | copy-start | bytes 516100
  279.4 4.8 %copy-start.16 = (f32[1,32,1,1344]{3,1,2,0:T(8,128)S(1)}, f32[1,32,1,1344]{3,1,2,0:T(8,128)}, u32[]{:S(2)}) copy-start(f32[1,32,1,1344]{3,1,2,0:T(8,128)} %copy.115) | copy-start | bytes 516100
  279.4 4.8 %copy-start.30 = (f32[1344]{0:T(1024)S(1)}, f32[1344]{0:T(1024)}, u32[]{:S(2)}) copy-start(f32[1344]{0:T(1024)} %param.12) | copy-start | bytes 16132
  284.2 8.5 %copy-start.2 = (f32[1,256,1344]{2,1,0:T(8,128)S(1)}, f32[1,256,1344]{2,1,0:T(8,128)}, u32[]{:S(2)}) copy-start(f32[1,256,1344]{2,1,0:T(8,128)} %copy.77) | copy-start | bytes 4128772
  284.2 8.4 %copy-start.9 = (bf16[1,256,1344]{2,1,0:T(8,128)(2,1)S(1)}, bf16[1,256,1344]{2,1,0:T(8,128)(2,1)}, u32[]{:S(2)}) copy-start(bf16[1,256,1344]{2,1,0:T(8,128)(2,1)} %copy.78) | copy-start | bytes 2064388
  284.2 8.4 %copy-start.32 = (f32[1344]{0:T(1024)S(1)}, f32[1344]{0:T(1024)}, u32[]{:S(2)}) copy-start(f32[1344]{0:T(1024)} %param.13) | copy-start | bytes 16132
  292.7 3.6 copy-start.5
  306.9 3.1 copy-start.3
  306.9 3.1 copy-start.33
  310.0 5.5 %copy-start.34 = (f32[1344]{0:T(1024)S(1)}, f32[1344]{0:T(1024)}, u32[]{:S(2)}) copy-start(f32[1344]{0:T(1024)} %get-tuple-element.75) | copy-start | bytes 16132
  310.0 5.5 %copy-start.35 = (f32[1344]{0:T(1024)S(1)}, f32[1344]{0:T(1024)}, u32[]{:S(2)}) copy-start(f32[1344]{0:T(1024)} %get-tuple-element.80) | copy-start | bytes 16132
  310.0 5.5 %copy-start.36 = (f32[1344]{0:T(1024)S(1)}, f32[1344]{0:T(1024)}, u32[]{:S(2)}) copy-start(f32[1344]{0:T(1024)} %get-tuple-element.81) | copy-start | bytes 16132
  313.3 35.2 %copy-start.37 = (f32[1344]{0:T(1024)S(1)}, f32[1344]{0:T(1024)}, u32[]{:S(2)}) copy-start(f32[1344]{0:T(1024)} %param.14) | copy-start | bytes 16132
  (14 other events, 18.5 us)
Sparse Core Ops, SparseCore 0:
  304.2 98.5 all-reduce.47
where the time goes:
time: 422 us; the launch traced here: 415 us
  local copies, waits for them, and re-layouts  187 us (44%)
  other arithmetic  109 us (26%)
  waiting for transfers between devices  53.7 us (13%)
  blocking collectives  40.5 us (10%)
  between operations  14.7 us (3%)
  matrix products  8.07 us (2%)
    pad x16, local copies, waits for them, and re-layouts, shards(): lax.associative_scan(combine, (group_prod, group_state), axis=1)  64.3 us
    psum x1, waiting for transfers between devices, shards(): lax.psum((local_a, local_x, bias_ga, bias_gx, decay_g), ('seq', 'dp'))  53.6 us
    pad x16, local copies, waits for them, and re-layouts, shards(): lax.associative_scan(combine, (group_prod, group_grad), reverse=True, axi...  53.6 us
    unnamed x98, local copies, waits for them, and re-layouts  41.1 us
    psum x1, blocking collectives, shards(): lax.psum((local_a, local_x, bias_ga, bias_gx, decay_g), ('seq', 'dp'))  33 us
    dot_general x1, other arithmetic, shards(): jnp.einsum('bntsc,bnsc->bntc', factor, drive.reshape(batch, groups, span_...  15.7 us
    add x10, other arithmetic, shards(): lax.associative_scan(combine, (group_prod, group_state), axis=1)  11.8 us
    add x10, other arithmetic, shards(): lax.associative_scan(combine, (group_prod, group_grad), reverse=True, axi...  10.7 us
  transfers between devices with their start and end apart: 2, of which 1 were waited for; matrix products, arithmetic and copies ran while one was open for 8% of the time, Pallas kernels for 0%

commit v1 on v0

--- a/solution.py
+++ b/solution.py
@@ -125,7 +125,7 @@
     bias_gx = jnp.sum(dpre_x, (0, 1))
     decay_g = jnp.sum(-8.0 * rate * wsum, (0, 1))
     grad_a, grad_x, bias_ga, bias_gx, decay_g = lax.psum(
-        (local_a, local_x, bias_ga, bias_gx, decay_g), ("seq", "dp")
+        lax.psum((local_a, local_x, bias_ga, bias_gx, decay_g), "dp"), "seq"
     )
     return (input_grad, grad_a, grad_x, bias_ga, bias_gx, jax.nn.sigmoid(decay_param) * decay_g)
 

time: 422 us -> 510 us (1.21)
  waiting for transfers between devices: 53.7 us -> 155 us
  blocking collectives: 40.5 us -> 27.7 us
    psum x1 -> x2, waiting for transfers between devices: 53.6 us -> 155 us  [the longest x1 155 us: shards(): lax.psum((local_a, local_x, bias_ga, bias_gx, decay_g), 'dp')]
    psum x1 -> x2, blocking collectives: 33 us -> 20.2 us  [the longest x1 16.2 us: shards(): lax.psum((local_a, local_x, bias_ga, bias_gx, decay_g), 'dp')]
    unnamed x98 -> x100, local copies, waits for them, and re-layouts: 41.1 us -> 40.3 us
  transfers between devices with their start and end apart: 2 -> 3, of which waited for: 1 -> 1; matrix products, arithmetic and copies ran while one was open for 8% -> 7% of each run, Pallas kernels for 0% -> 0%
where the time goes in v1:
time: 510 us; the launch traced here: 504 us
  local copies, waits for them, and re-layouts  186 us (36%)
  waiting for transfers between devices  155 us (30%)
  other arithmetic  109 us (21%)
  blocking collectives  27.7 us (5%)
  between operations  14.7 us (3%)
  matrix products  8.04 us (2%)
    psum x1, waiting for transfers between devices, shards(): lax.psum((local_a, local_x, bias_ga, bias_gx, decay_g), 'dp')  155 us
    pad x16, local copies, waits for them, and re-layouts, shards(): lax.associative_scan(combine, (group_prod, group_state), axis=1)  64.3 us
    pad x16, local copies, waits for them, and re-layouts, shards(): lax.associative_scan(combine, (group_prod, group_grad), reverse=True, axi...  53.7 us
    unnamed x100, local copies, waits for them, and re-layouts  40.3 us
    psum x1, blocking collectives, shards(): lax.psum((local_a, local_x, bias_ga, bias_gx, decay_g), 'dp')  16.2 us
    dot_general x1, other arithmetic, shards(): jnp.einsum('bntsc,bnsc->bntc', factor, drive.reshape(batch, groups, span_...  15.7 us
    add x10, other arithmetic, shards(): lax.associative_scan(combine, (group_prod, group_state), axis=1)  11.8 us
    add x10, other arithmetic, shards(): lax.associative_scan(combine, (group_prod, group_grad), reverse=True, axi...  10.7 us
  transfers between devices with their start and end apart: 3, of which 1 were waited for; matrix products, arithmetic and copies ran while one was open for 7% of the time, Pallas kernels for 0%

profile of v1, /device:TPU:0, one launch (start us, length us, event | category | flops | bytes accessed | tf_op | source)
XLA Modules:
  0.0 503.6 jit_solution(14297077021866443657)
XLA Ops:
  28.7 6.4 %reduce_window_sum.23 = f32[1,32,8,1344]{3,2,1,0:T(8,128)S(1)} reduce-window(f32[1,32,8,1344]{3,2,1,0:T(8,128)} %divide_multiply_fusion, f32[]{:T(128)} %constant.20.clone.1), window={size=1x1x8x1 pad=0_0x0_0x7_0x0_0}, to_apply=%region_1.2 | reduce-window | flops 2408448 | bytes 2752516 | tf_op jit(solution)/shard_map/jit(cumsum)/reduce_window_sum | solution.py:68
  37.4 4.8 multiply_reduce_fusion.1
  48.1 15.7 %multiply_reduce_fusion = f32[32,1344,8]{1,2,0:T(8,128)S(1)} fusion(f32[32,1344,8]{1,2,0:T(8,128)S(1)} %fusion.6, f32[32,8,1344]{2,1,0:T(8,128)S(1)} %bitcast.112, pred[32,8,8]{2,1,0:T(8,128)(4,1)S(1)} %compare_and_fusion), kind=kLoop, calls=%fused_computation | loop fusion | flops 13418496 | bytes 4130816 | tf_op jit(solution)/shard_map/bntsc,bnsc->bntc/dot_general | solution.py:77
  87.3 3.2 pad.142
  95.0 3.2 pad.133
  98.2 3.2 pad.143
  127.9 3.2 pad.162
  132.4 3.2 pad.152
  135.6 3.2 pad.153
  138.8 3.2 pad.163
  147.9 4.7 pad.164
  154.0 4.7 pad.154
  158.7 4.7 pad.155
  163.4 4.7 pad.165
  172.7 5.5 %pad.307 = f32[1,31,1344]{2,0,1:T(1,128)} pad(f32[1,16,1344]{2,0,1:T(1,128)S(1)} %add.530, f32[]{:T(128)} %constant.20.clone.1), padding=0_0_0x0_0_1x0_0_0 | pad | bytes 252676
  178.3 5.6 %pad.167 = f32[1,32,1344]{2,0,1:T(1,128)} pad(f32[1,16,1344]{2,0,1:T(1,128)S(1)} %add.530, f32[]{:T(128)} %constant.20.clone.1), padding=0_0_0x1_0_1x0_0_0 | pad | bytes 258052 | tf_op jit(solution)/shard_map/pad | solution.py:97
  183.8 8.5 %pad.305 = f32[1,31,1344]{2,0,1:T(1,128)} pad(f32[1,16,1344]{2,0,1:T(1,128)} %add.524, f32[]{:T(128)} %constant.20.clone.1), padding=0_0_0x0_0_1x0_0_0 | pad | bytes 252676
  192.3 8.4 %pad.157 = f32[1,32,1344]{2,0,1:T(1,128)} pad(f32[1,16,1344]{2,0,1:T(1,128)} %add.524, f32[]{:T(128)} %constant.20.clone.1), padding=0_0_0x1_0_1x0_0_0 | pad | bytes 258052 | tf_op jit(solution)/shard_map/pad | solution.py:97
  201.9 5.5 %pad.309 = f32[1,31,1344]{2,0,1:T(1,128)} pad(f32[1,16,1344]{2,0,1:T(1,128)S(1)} %add.496, f32[]{:T(128)} %constant.20.clone.1), padding=0_0_0x0_0_1x0_0_0 | pad | bytes 252676
  207.5 5.6 %pad.137 = f32[1,32,1344]{2,0,1:T(1,128)} pad(f32[1,16,1344]{2,0,1:T(1,128)S(1)} %add.496, f32[]{:T(128)} %constant.20.clone.1), padding=0_0_0x1_0_1x0_0_0 | pad | bytes 258052 | tf_op jit(solution)/shard_map/pad | solution.py:98
  214.0 4.7 pad.145
  219.7 5.5 %pad.311 = f32[1,31,1344]{2,0,1:T(1,128)} pad(f32[1,16,1344]{2,0,1:T(1,128)S(1)} %add.502, f32[]{:T(128)} %constant.20.clone.1), padding=0_0_0x0_0_1x0_0_0 | pad | bytes 252676
  225.2 5.6 %pad.147 = f32[1,32,1344]{2,0,1:T(1,128)} pad(f32[1,16,1344]{2,0,1:T(1,128)S(1)} %add.502, f32[]{:T(128)} %constant.20.clone.1), padding=0_0_0x1_0_1x0_0_0 | pad | bytes 258052 | tf_op jit(solution)/shard_map/pad | solution.py:98
  231.8 5.6 %pad.156 = f32[1,32,1344]{2,0,1:T(1,128)} pad(f32[1,16,1344]{2,0,1:T(1,128)S(1)} %pad_maximum_fusion.2, f32[]{:T(128)} %constant.20.clone.1), padding=0_0_0x0_1_1x0_0_0 | pad | bytes 258052 | tf_op jit(solution)/shard_map/pad | solution.py:97
  238.3 5.5 %pad.166 = f32[1,32,1344]{2,0,1:T(1,128)} pad(f32[1,16,1344]{2,0,1:T(1,128)S(1)} %pad_maximum_fusion.3, f32[]{:T(128)} %constant.20.clone.1), padding=0_0_0x0_1_1x0_0_0 | pad | bytes 258052 | tf_op jit(solution)/shard_map/pad | solution.py:97
  247.1 8.4 %pad.146 = f32[1,32,1344]{2,0,1:T(1,128)} pad(f32[1,16,1344]{2,0,1:T(1,128)} %pad_maximum_fusion.1, f32[]{:T(128)} %constant.20.clone.1), padding=0_0_0x0_1_1x0_0_0 | pad | bytes 258052 | tf_op jit(solution)/shard_map/pad | solution.py:98
  257.2 8.4 %pad.136 = f32[1,32,1344]{2,0,1:T(1,128)} pad(f32[1,16,1344]{2,0,1:T(1,128)} %pad_maximum_fusion, f32[]{:T(128)} %constant.20.clone.1), padding=0_0_0x0_1_1x0_0_0 | pad | bytes 258052 | tf_op jit(solution)/shard_map/pad | solution.py:98
  284.5 7.3 %fusion.15 = (f32[1344]{0:T(1024)}, f32[1,256,1344]{2,1,0:T(8,128)S(1)}, f32[1344]{0:T(1024)}, f32[1344]{0:T(1024)}, f32[1,256,1344]{2,1,0:T(8,128)}) fusion(bf16[1,256,1344]{2,1,0:T(8,128)(2,1)} %copy.78, f32[1,256,1344]{2,1,0:T(8,128)} %copy.77, f32[1344]{0:T(1024)} %param.13, f32[1344]{0:T(1024)S(1)} %fusion.19, f32[1,256,1344]{2,1,0:T(8,128)} %copy.75, ...), kind=kLoop, calls=%fused_computation.84 | loop fusion | flops 15134784 | bytes 10873600 | tf_op jit(solution)/shard_map/reduce_sum | solution.py:125
  304.3 155.0 %all-reduce.51.cloned.1.call-done = (f32[4,336,336]{1,2,0:T(8,128)}, f32[4,336,336]{1,2,0:T(8,128)}) async-done(((f32[4,336,336]{1,2,0:T(8,128)}, f32[4,336,336]{1,2,0:T(8,128)}), (f32[4,336,336]{1,2,0:T(8,128)}, f32[4,336,336]{1,2,0:T(8,128)})) %all-reduce.51.cloned.1.call-update) | async-done | bytes 3612688 | tf_op jit(solution)/shard_map/psum | solution.py:128
  465.3 3.3 add_convert_fusion
  471.0 16.2 %all-reduce.44 = (f32[1344]{0:T(1024)S(1)}, f32[1344]{0:T(1024)S(1)}, f32[1344]{0:T(1024)S(1)}) all-reduce(f32[1344]{0:T(1024)S(1)} %copy-done.36, f32[1344]{0:T(1024)S(1)} %copy-done.35, f32[1344]{0:T(1024)S(1)} %copy-done.37), channel_id=1, replica_groups=mesh['seq'=2,'width'=4,'dp'=4] {'dp'}, use_global_device_ids=true, to_apply=%region_7.8 | all-reduce | flops 4032 | bytes 32256 | tf_op jit(solution)/shard_map/psum | solution.py:128
  487.3 4.0 all-reduce.46
  (230 shorter events, 152.1 us)
Async XLA Ops:
  7.2 9.0 %copy-start = (bf16[4,336,336]{2,1,0:T(8,128)(2,1)S(1)}, bf16[4,336,336]{2,1,0:T(8,128)(2,1)}, u32[]{:S(2)}) copy-start(bf16[4,336,336]{2,1,0:T(8,128)(2,1)} %param.10) | copy-start | bytes 2709508
  7.2 7.4 %copy-start.22 = (bf16[1,256,1344]{1,2,0:T(8,128)(2,1)S(1)}, bf16[1,256,1344]{1,2,0:T(8,128)(2,1)}, u32[]{:S(2)}) copy-start(bf16[1,256,1344]{1,2,0:T(8,128)(2,1)} %param.9) | copy-start | bytes 2064388
  7.2 452.2 %all-reduce.51.cloned.1.call-start = ((), (), s32[]{:S(2)}) async-start(), calls=%async_computation | async-start | bytes 8257536 | tf_op jit(solution)/shard_map/psum | solution.py:128
  8.6 27.3 %collective-permute-start = (s32[1,1]{1,0:T(1,128)}, s32[1,1]{1,0:T(1,128)}, u32[]{:S(2)}, u32[]{:S(2)}) collective-permute-start(s32[1,1]{1,0:T(1,128)} %slice.468), channel_id=1, source_target_pairs={{0,16},{1,17},{2,18},{3,19},{4,20},{5,21},{6,22},{7,23},{8,24},{9,... | collective-permute-start | bytes 20 | tf_op jit(solution)/shard_map/ppermute | solution.py:10
  28.7 7.3 %copy-start.42 = (s32[1,256]{1,0:T(1,128)S(1)}, s32[1,256]{1,0:T(1,128)}, u32[]{:S(2)}) copy-start(s32[1,256]{1,0:T(1,128)} %param.15) | copy-start | bytes 3076
  36.7 9.0 %copy-start.41 = (f32[1,256]{1,0:T(1,128)}, f32[1,256]{1,0:T(1,128)S(1)}, u32[]{:S(2)}) copy-start(f32[1,256]{1,0:T(1,128)S(1)} %get-tuple-element.83) | copy-start | bytes 3076
  37.4 9.1 %copy-start.1 = (f32[1,256,1344]{2,1,0:T(8,128)S(1)}, f32[1,256,1344]{2,1,0:T(8,128)}, u32[]{:S(2)}) copy-start(f32[1,256,1344]{2,1,0:T(8,128)} %copy.77) | copy-start | bytes 4128772
  37.4 9.1 %copy-start.4 = (f32[1,256,1344]{2,1,0:T(8,128)S(1)}, f32[1,256,1344]{2,1,0:T(8,128)}, u32[]{:S(2)}) copy-start(f32[1,256,1344]{2,1,0:T(8,128)} %copy.75) | copy-start | bytes 4128772
  37.4 9.1 %copy-start.32 = (f32[1344]{0:T(1024)S(1)}, f32[1344]{0:T(1024)}, u32[]{:S(2)}) copy-start(f32[1344]{0:T(1024)} %param.13) | copy-start | bytes 16132
  42.2 4.3 copy-start.8
  45.0 3.1 copy-start.16
  112.7 39.9 %copy-start.40 = (f32[1,1,1344]{2,0,1:T(1,128)S(1)}, f32[1,1,1344]{2,0,1:T(1,128)}, u32[]{:S(2)}) copy-start(f32[1,1,1344]{2,0,1:T(1,128)} %slice.512) | copy-start | bytes 16132
  171.7 30.0 %copy-start.29 = (f32[1,8,1344]{2,0,1:T(1,128)S(1)}, f32[1,8,1344]{2,0,1:T(1,128)}, u32[]{:S(2)}) copy-start(f32[1,8,1344]{2,0,1:T(1,128)} %add.494) | copy-start | bytes 129028
  171.7 41.4 %copy-start.39 = (f32[1,1,1344]{2,0,1:T(1,128)S(1)}, f32[1,1,1344]{2,0,1:T(1,128)}, u32[]{:S(2)}) copy-start(f32[1,1,1344]{2,0,1:T(1,128)} %slice.496) | copy-start | bytes 16132
  218.7 36.9 %slice-start = ((f32[1,32,1344]{2,0,1:T(1,128)}), f32[1,1,1344]{2,0,1:T(1,128)S(1)}, s32[]{:S(2)}) async-start(f32[1,32,1344]{2,0,1:T(1,128)} %copy-done.16), calls=%async_computation.2 | async-start | bytes 11264 | tf_op jit(solution)/shard_map/slice | solution.py:98
  245.7 31.7 %copy-start.18 = (f32[1,32,1344]{2,0,1:T(1,128)S(1)}, f32[1,32,1344]{2,0,1:T(1,128)}, u32[]{:S(2)}) copy-start(f32[1,32,1344]{2,0,1:T(1,128)} %pad.167) | copy-start | bytes 516100
  245.7 32.8 %copy-start.19 = (f32[1,32,1344]{2,0,1:T(1,128)S(1)}, f32[1,32,1344]{2,0,1:T(1,128)}, u32[]{:S(2)}) copy-start(f32[1,32,1344]{2,0,1:T(1,128)} %pad.157) | copy-start | bytes 516100
  269.1 10.9 %copy-start.20 = (f32[1,32,1344]{2,0,1:T(1,128)S(1)}, f32[1,32,1344]{2,0,1:T(1,128)}, u32[]{:S(2)}) copy-start(f32[1,32,1344]{2,0,1:T(1,128)} %pad.147) | copy-start | bytes 516100
  269.1 10.9 %copy-start.21 = (f32[1,32,1344]{2,0,1:T(1,128)S(1)}, f32[1,32,1344]{2,0,1:T(1,128)}, u32[]{:S(2)}) copy-start(f32[1,32,1344]{2,0,1:T(1,128)} %pad.146) | copy-start | bytes 516100
  279.6 4.8 copy-start.17
  279.6 4.8 copy-start.31
  284.5 8.4 %copy-start.2 = (f32[1,256,1344]{2,1,0:T(8,128)S(1)}, f32[1,256,1344]{2,1,0:T(8,128)}, u32[]{:S(2)}) copy-start(f32[1,256,1344]{2,1,0:T(8,128)} %copy.77) | copy-start | bytes 4128772
  284.5 8.4 %copy-start.9 = (bf16[1,256,1344]{2,1,0:T(8,128)(2,1)S(1)}, bf16[1,256,1344]{2,1,0:T(8,128)(2,1)}, u32[]{:S(2)}) copy-start(bf16[1,256,1344]{2,1,0:T(8,128)(2,1)} %copy.78) | copy-start | bytes 2064388
  284.5 8.4 %copy-start.33 = (f32[1344]{0:T(1024)S(1)}, f32[1344]{0:T(1024)}, u32[]{:S(2)}) copy-start(f32[1344]{0:T(1024)} %param.13) | copy-start | bytes 16132
  292.9 3.6 copy-start.5
  304.3 187.6 %all-reduce.53.cloned.1.call-start = ((), (), s32[]{:S(2)}) async-start(), calls=%async_computation.1 | async-start | bytes 8257536 | tf_op jit(solution)/shard_map/psum | solution.py:127
  462.2 3.0 copy-start.34
  465.2 5.8 %copy-start.35 = (f32[1344]{0:T(1024)S(1)}, f32[1344]{0:T(1024)}, u32[]{:S(2)}) copy-start(f32[1344]{0:T(1024)} %get-tuple-element.80) | copy-start | bytes 16132
  465.2 5.8 %copy-start.36 = (f32[1344]{0:T(1024)S(1)}, f32[1344]{0:T(1024)}, u32[]{:S(2)}) copy-start(f32[1344]{0:T(1024)} %get-tuple-element.85) | copy-start | bytes 16132
  465.3 5.8 %copy-start.37 = (f32[1344]{0:T(1024)S(1)}, f32[1344]{0:T(1024)}, u32[]{:S(2)}) copy-start(f32[1344]{0:T(1024)} %get-tuple-element.86) | copy-start | bytes 16132
  468.6 22.7 %copy-start.38 = (f32[1344]{0:T(1024)S(1)}, f32[1344]{0:T(1024)}, u32[]{:S(2)}) copy-start(f32[1344]{0:T(1024)} %param.14) | copy-start | bytes 16132
  491.9 3.1 copy-start.15
  (16 other events, 23.8 us)
Sparse Core Ops, SparseCore 0:
  304.4 154.9 all-reduce.50
  462.0 27.2 all-reduce.52
